TPU v7x, 32 devices: a whole 2x2x4 slice. The times are simulated.
32 devices in a mesh: dp: 4 (over x, core), mp: 8 (over z, y).
Axes of the slice: x: 2, y: 2, z: 4, core: 2. Of those that a mesh axis runs over, the one named last changes fastest.
Arguments:
- tokens: bfloat16 [1280, 1792], P(('dp', 'mp')), may hold values from -6 to 6
- norm_gain: float32 [1792], replicated, may hold values from 0.5 to 1.5
- norm_bias: float32 [1792], replicated, may hold values from -3 to 3
- w_in: bfloat16 [1792, 15360], P('dp', 'mp'), may hold values from -0.125 to 0.125
- b_in: float32 [15360], P('mp'), may hold values from -3 to 3
- w_out: bfloat16 [15360, 1792], P('mp', 'dp'), may hold values from -0.046875 to 0.046875
- b_out: float32 [1792], replicated, may hold values from -3 to 3
Outputs:
- result: bfloat16 [1280, 1792], P(('dp', 'mp'))
All inputs are finite; a program needn't handle non-finite values.
Results may differ from a plain program's by a relative error of at most 0.0042.
Values may be sent and summed in bfloat16 or wider, within the bound.
A program may use at most 128 MiB of HBM per device.

v0:
```python
import jax
import jax.numpy as jnp
from jax import lax
from jax.sharding import PartitionSpec as P


def on_device(tokens, norm_gain, norm_bias, w_in, b_in, w_out, b_out):
    values = tokens.astype(jnp.float32)
    center = jnp.mean(values, axis=1, keepdims=True)
    spread = jnp.mean((values - center) ** 2, axis=1, keepdims=True)
    normed = ((values - center) / jnp.sqrt(spread + 1e-06) * norm_gain + norm_bias).astype(
        jnp.bfloat16
    )
    w_in_full = lax.all_gather(w_in, "dp", axis=0, tiled=True)
    gathered = lax.all_gather(normed, "mp", axis=0, tiled=True)
    pre = jnp.dot(gathered, w_in_full, preferred_element_type=jnp.float32) + b_in
    hidden = jax.nn.gelu(pre, approximate=False).astype(jnp.bfloat16)
    w_out_full = lax.all_gather(w_out, "dp", axis=1, tiled=True)
    summed = lax.psum_scatter(
        jnp.dot(hidden, w_out_full, preferred_element_type=jnp.float32),
        "mp",
        scatter_dimension=0,
        tiled=True,
    )
    return (values + summed + b_out).astype(jnp.bfloat16)


def solution(mesh):
    placed = (P(("dp", "mp"), None), P(), P(), P("dp", "mp"), P("mp"), P("mp", "dp"), P())
    return jax.shard_map(
        on_device, mesh=mesh, in_specs=placed, out_specs=P(("dp", "mp"), None), check_vma=False
    )
```

profile of v0, /device:TPU:0, one launch (start us, length us, event | category | flops | bytes accessed | tf_op | source)
XLA Modules:
  0.0 249.3 jit_solution(16586171305829466705)
XLA Ops:
  6.5 0.0 copy-start.2
  6.5 0.0 all-gather.4.cloned.1.call-start
  6.5 1.0 convert_reduce_fusion
  7.6 1.1 fusion.45
  8.7 1.7 fusion.48
  10.5 0.0 all-gather.4.cloned.1.call-update
  10.5 0.0 all-gather.6.cloned.1.call-start
  10.5 0.7 all-gather.6.cloned.1.call-update
  11.2 0.0 all-gather.8.cloned.1.call-start
  11.3 0.7 all-gather.8.cloned.1.call-update
  12.0 0.0 copy-start
  12.0 0.0 copy-start.1
  12.0 0.0 reduce-scatter.2.cloned.1.call-start
  12.0 42.5 %all-gather.4.cloned.1.call-done = bf16[320,1792]{1,0:T(8,128)(2,1)} async-done(((bf16[40,1792]{1,0:T(8,128)(2,1)}), bf16[320,1792]{1,0:T(8,128)(2,1)}) %all-gather.4.cloned.1.call-update) | async-done | bytes 1146896 | tf_op jit(solution)/shard_map/all_gather | solution.py:15
  54.6 49.7 %all-gather.6.cloned.1.call-done = bf16[1792,1920]{1,0:T(8,128)(2,1)} async-done(((bf16[448,1920]{1,0:T(8,128)(2,1)}), bf16[1792,1920]{1,0:T(8,128)(2,1)}) %all-gather.6.cloned.1.call-update) | async-done | bytes 6881296 | tf_op jit(solution)/shard_map/all_gather | solution.py:14
  104.3 51.3 %all-gather.8.cloned.1.call-done = bf16[1920,1792]{0,1:T(8,128)(2,1)} async-done(((bf16[1920,448]{0,1:T(8,128)(2,1)}), bf16[1920,1792]{0,1:T(8,128)(2,1)}) %all-gather.8.cloned.1.call-update) | async-done | bytes 6881296 | tf_op jit(solution)/shard_map/all_gather | solution.py:18
  155.6 0.0 copy-done.2
  155.6 15.7 %fusion.10 = f32[320,1792]{1,0:T(8,128)} fusion(bf16[1920,1792]{0,1:T(8,128)(2,1)} %all-gather.8.cloned.1.call-done, bf16[320,1792]{1,0:T(8,128)(2,1)} %all-gather.4.cloned.1.call-done, bf16[1792,1920]{1,0:T(8,128)(2,1)} %all-gather.6.cloned.1.call-done, f32[1920]{0:T(1024)S(1)} %copy-done.2), kind=kOutput, calls=%fused_computation.20 | convolution fusion | flops 4444569600 | bytes 17210880 | tf_op jit(solution)/shard_map/dot_general | solution.py:20
  171.3 0.0 reduce-scatter.2.cloned.1.call-update
  171.4 69.7 %reduce-scatter.2.cloned.1.call-done = f32[40,1792]{1,0:T(8,128)} async-done(((f32[320,1792]{1,0:T(8,128)}), f32[40,1792]{1,0:T(8,128)}) %reduce-scatter.2.cloned.1.call-update) | async-done | bytes 286736 | tf_op jit(solution)/shard_map/reduce_scatter | solution.py:19
  241.1 0.0 copy-done
  241.1 0.0 copy-done.1
  241.1 1.7 fusion.50
  (2 shorter events, 0.0 us)
Async XLA Ops:
  6.5 149.1 %copy-start.2 = (f32[1920]{0:T(1024)S(1)}, f32[1920]{0:T(1024)}, u32[]{:S(2)}) copy-start(f32[1920]{0:T(1024)} %param.11) | copy-start | bytes 23044
  6.5 48.0 %all-gather.4.cloned.1.call-start = ((), (), s32[]{:S(2)}) async-start(), calls=%async_computation.1 | async-start | bytes 1290240 | tf_op jit(solution)/shard_map/all_gather | solution.py:15
  10.5 93.8 %all-gather.6.cloned.1.call-start = ((), (), s32[]{:S(2)}) async-start(), calls=%async_computation.2 | async-start | bytes 8601600 | tf_op jit(solution)/shard_map/all_gather | solution.py:14
  11.2 144.4 %all-gather.8.cloned.1.call-start = ((), (), s32[]{:S(2)}) async-start(), calls=%async_computation.3 | async-start | bytes 8601600 | tf_op jit(solution)/shard_map/all_gather | solution.py:18
  12.0 229.1 %copy-start = (bf16[40,1792]{1,0:T(8,128)(2,1)S(1)}, bf16[40,1792]{1,0:T(8,128)(2,1)}, u32[]{:S(2)}) copy-start(bf16[40,1792]{1,0:T(8,128)(2,1)} %param.7) | copy-start | bytes 430084
  12.0 229.1 %copy-start.1 = (f32[1792]{0:T(1024)S(1)}, f32[1792]{0:T(1024)}, u32[]{:S(2)}) copy-start(f32[1792]{0:T(1024)} %param.13) | copy-start | bytes 21508
  12.0 229.1 %reduce-scatter.2.cloned.1.call-start = ((), (), s32[]{:S(2)}) async-start(), calls=%async_computation.4 | async-start | bytes 2580480 | tf_op jit(solution)/shard_map/reduce_scatter | solution.py:19
Sparse Core Ops, SparseCore 0:
  10.6 43.9 all-gather.3
  56.1 48.1 all-gather.5
  105.9 49.6 all-gather.7
  171.5 69.5 reduce-scatter.1
where the time goes:
time: 249 us
  waiting for transfers between devices  215 us (86%)
  matrix products  15.7 us (6%)
  between operations  13.2 us (5%)
  other arithmetic  5.56 us (2%)
    reduce_scatter x1, waiting for transfers between devices, on_device(): lax.psum_scatter(jnp.dot(hidden, w_out_full, preferred_element_type=jnp.f...  69.7 us
    all_gather x1, waiting for transfers between devices, on_device(): w_out_full = lax.all_gather(w_out, 'dp', axis=1, tiled=True)  51.3 us
    all_gather x1, waiting for transfers between devices, on_device(): w_in_full = lax.all_gather(w_in, 'dp', axis=0, tiled=True)  49.7 us
    all_gather x1, waiting for transfers between devices, on_device(): gathered = lax.all_gather(normed, 'mp', axis=0, tiled=True)  42.5 us
    dot_general x1, matrix products, on_device(): jnp.dot(hidden, w_out_full, preferred_element_type=jnp.float32)  15.7 us
  transfers between devices with their start and end apart: 4, of which 4 were waited for; matrix products, arithmetic and copies ran while one was open for 0% of the time, Pallas kernels for 0%

commit v1 on v0

v1 whole, which is shorter than its diff:
```python
import functools

import jax
import jax.numpy as jnp
from jax import lax
from jax.experimental import pallas as pl
from jax.experimental.pallas import tpu as pltpu
from jax.sharding import PartitionSpec as P

MESH = pl.DeviceIdType.MESH
LANES = 128
VMEM_GRANT = 60 * 2**20


def flip(index, mask, size):
    out, bit = index, 1
    while bit < size:
        if mask & bit:
            out = out + bit - 2 * bit * (lax.rem(lax.div(index, bit), 2))
        bit *= 2
    return out


def gelu(pre):
    return 0.5 * pre * (1.0 + lax.erf(pre * (0.5**0.5)))


def kernel(
    lines, tokens, gain, bias, w_in, b_in, w_out, b_out, out,
    shift, tok, win, wout, normed, hidden, part, own, from_y, sums, from_z, to_x, kept, from_x,
    tok_sem, win_sem, wout_sem, y_sem, z_sem, x_sem, local_sem, send_sem,
):
    dp, mp = lax.axis_index("dp"), lax.axis_index("mp")
    x, core = lax.div(dp, 2), lax.rem(dp, 2)
    z, y = lax.div(mp, 2), lax.rem(mp, 2)
    ox, oy = 1 - x, 1 - y
    rows, depth = tokens.shape[0], w_in.shape[0]
    units = w_in.shape[1]
    half = units // 2
    start = half // LANES * LANES
    width = units - start
    x_dev = (2 * ox + core, mp)
    core_dev = (2 * x + 1 - core, mp)
    y_dev = (dp, 2 * z + oy)
    z_at = [flip(z, k, lines) for k in range(lines)]
    z_dev = [(dp, 2 * z_at[k] + y) for k in range(lines)]

    barrier = pltpu.get_barrier_semaphore()
    partners = [x_dev, core_dev, y_dev] + z_dev[1:]
    for partner in partners:
        pl.semaphore_signal(barrier, inc=1, device_id=partner, device_id_type=MESH)
    pl.semaphore_wait(barrier, len(partners))

    sends = []

    def send(src, dst, sem, device):
        copy = pltpu.make_async_remote_copy(
            src_ref=src, dst_ref=dst, send_sem=send_sem.at[len(sends)], recv_sem=sem,
            device_id=device, device_id_type=MESH,
        )
        copy.start()
        sends.append(copy)

    def arrive(dst, sem):
        pltpu.make_async_remote_copy(
            src_ref=dst, dst_ref=dst, send_sem=send_sem.at[0], recv_sem=sem,
            device_id=x_dev, device_id_type=MESH,
        ).wait_recv()

    def slot(yy, zz, side):
        return (yy * lines + zz) * 2 + side

    mine = tok.at[slot(y, z, x)]
    mine_sem = tok_sem.at[y, z, x]
    send(tokens, mine, mine_sem, x_dev)
    for k in range(1, lines):
        send(tokens, mine, mine_sem, z_dev[k])
    send(tokens, mine, mine_sem, y_dev)
    locals_ = [pltpu.make_async_copy(tokens, mine, local_sem.at[0])]

    def columns(weight, side):
        return weight.at[:, pl.ds(pl.multiple_of(side * start, LANES), width)]


    def rows_of(full, owner):
        return full.at[pl.ds(pl.multiple_of(owner * depth, 16), depth), :]

    far, near, across = 2 * ox + core, 2 * x + 1 - core, 2 * ox + 1 - core
    send(columns(w_in, ox), rows_of(win, dp), win_sem.at[dp], x_dev)
    send(columns(w_in, x), rows_of(win, dp), win_sem.at[dp], core_dev)
    send(columns(w_out, ox), rows_of(wout, dp), wout_sem.at[dp], x_dev)
    send(columns(w_out, x), rows_of(wout, dp), wout_sem.at[dp], core_dev)
    locals_.append(pltpu.make_async_copy(columns(w_in, x), rows_of(win, dp), local_sem.at[1]))
    locals_.append(pltpu.make_async_copy(columns(w_out, x), rows_of(wout, dp), local_sem.at[2]))
    for copy in locals_:
        copy.start()

    shift[...] = jnp.broadcast_to(b_in[...], shift.shape)

    arrive(tok.at[slot(y, z, ox)], tok_sem.at[y, z, ox])
    for k in range(1, lines):
        send(tok.at[slot(y, z, ox)], tok.at[slot(y, z, ox)], tok_sem.at[y, z, ox], z_dev[k])
    send(tok.at[slot(y, z, ox)], tok.at[slot(y, z, ox)], tok_sem.at[y, z, ox], y_dev)
    for side in (x, ox):
        for k in range(1, lines):
            block, sem = tok.at[slot(y, z_at[k], side)], tok_sem.at[y, z_at[k], side]
            arrive(block, sem)
            send(block, block, sem, y_dev)

    def normalise(yy, zz):
        pair = jnp.concatenate(
            [tok[slot(yy, zz, 0)].astype(jnp.float32), tok[slot(yy, zz, 1)].astype(jnp.float32)], axis=0
        )
        center = jnp.mean(pair, axis=1, keepdims=True)
        spread = jnp.mean((pair - center) ** 2, axis=1, keepdims=True)
        value = (pair - center) / jnp.sqrt(spread + 1e-06) * gain[...] + bias[...]
        normed[yy, pl.ds(pl.multiple_of(zz * 2 * rows, 16), 2 * rows), :] = value.astype(
            normed.dtype
        )

    tile = 2 * LANES if width % (2 * LANES) == 0 else LANES

    def first(yy):
        def step(n, carry):
            at = pl.ds(pl.multiple_of(n * tile, LANES), tile)
            pre = jnp.dot(normed[yy], win[:, at], preferred_element_type=jnp.float32)
            pre = pre + shift[:1, pl.ds(pl.multiple_of(x * start + n * tile, LANES), tile)]
            unit = x * start + n * tile + lax.broadcasted_iota(jnp.int32, pre.shape, 1)
            keep = (unit >= x * half) & (unit < (x + 1) * half)
            hidden[yy, :, at] = jnp.where(keep, gelu(pre), 0.0).astype(hidden.dtype)
            return carry

        lax.fori_loop(0, width // tile, step, 0)

    locals_[0].wait()

    def norm_own(zz, carry):
        normalise(y, zz)
        return carry

    lax.fori_loop(0, lines, norm_own, 0)

    arrive(rows_of(win, far), win_sem.at[far])
    send(rows_of(win, far), rows_of(win, far), win_sem.at[far], core_dev)
    locals_[1].wait()
    arrive(rows_of(win, near), win_sem.at[near])
    arrive(rows_of(win, across), win_sem.at[across])
    first(y)

    for k in range(lines):
        for side in (x, ox):
            arrive(tok.at[slot(oy, z_at[k], side)], tok_sem.at[oy, z_at[k], side])
        normalise(oy, z_at[k])
    first(oy)

    def second(q, yy, zz):
        side = x if q == 0 else ox
        act = hidden[yy, pl.ds(pl.multiple_of(zz * 2 * rows, 16), 2 * rows), :]
        weight = wout[pl.ds(pl.multiple_of(side * 2 * depth, 16), 2 * depth), :]
        return lax.dot_general(
            act, weight, (((1,), (1,)), ((), ())), preferred_element_type=jnp.float32
        )

    def product(q):
        for k in range(lines):
            part[q, z_at[k]] = second(q, oy, z_at[k]).astype(part.dtype)
            send(part.at[q, z_at[k]], from_y.at[q, z_at[k]], y_sem.at[q, z_at[k]], y_dev)

        def step(zz, carry):
            own[q, zz] = second(q, y, zz)
            return carry

        lax.fori_loop(0, lines, step, 0)

    def along_z(q):
        for k in list(range(1, lines)) + [0]:
            at = z_at[k]
            arrive(from_y.at[q, at], y_sem.at[q, at])
            total = own[q, at] + from_y[q, at].astype(jnp.float32)
            if k:
                sums[q, at] = total.astype(sums.dtype)
                send(sums.at[q, at], from_z.at[q, z], z_sem.at[q, z], z_dev[k])
            else:
                own[q, at] = total

    def along_x(q):
        side = x if q == 0 else ox
        total = own[q, z]
        for k in range(1, lines):
            arrive(from_z.at[q, z_at[k]], z_sem.at[q, z_at[k]])
            total = total + from_z[q, z_at[k]].astype(jnp.float32)
        own[q, z] = total
        to_x[q] = own[q, z, pl.ds(pl.multiple_of(ox * rows, 8), rows), :].astype(to_x.dtype)
        send(to_x.at[q], from_x.at[side], x_sem.at[side], x_dev)
        kept[side] = own[q, z, pl.ds(pl.multiple_of(x * rows, 8), rows), :]

    locals_[2].wait()
    arrive(rows_of(wout, near), wout_sem.at[near])
    product(0)
    arrive(rows_of(wout, far), wout_sem.at[far])
    send(rows_of(wout, far), rows_of(wout, far), wout_sem.at[far], core_dev)
    along_z(0)
    arrive(rows_of(wout, across), wout_sem.at[across])
    product(1)
    along_x(0)
    along_z(1)
    along_x(1)
    columns_of, added = 2 * depth, b_out[...]
    for side in range(2):
        at = slice(side * columns_of, (side + 1) * columns_of)
        arrive(from_x.at[side], x_sem.at[side])
        total = kept[side] + from_x[side].astype(jnp.float32)
        out[:, at] = tok[slot(y, z, x), :, at].astype(jnp.float32) + total + added[:, at]
    for copy in sends:
        copy.wait_send()


def fused(mp, tokens, gain, bias, w_in, b_in, w_out, b_out):
    rows, dim = tokens.shape
    depth, units = w_in.shape
    lines = mp // 2
    width = units - units // 2 // LANES * LANES
    columns = 2 * depth
    bf16, f32, dma = jnp.bfloat16, jnp.float32, pltpu.SemaphoreType.DMA
    vmem = pl.BlockSpec(memory_space=pltpu.VMEM)
    hbm = pl.BlockSpec(memory_space=pl.ANY)
    n_sends = (lines + 1) * 2 + 4 + 2 * (lines - 1) + 2 + 2 * (lines + lines - 1 + 1)
    return pl.pallas_call(
        functools.partial(kernel, lines),
        out_shape=jax.ShapeDtypeStruct((rows, dim), f32),
        in_specs=[hbm, vmem, vmem, hbm, vmem, hbm, vmem],
        out_specs=vmem,
        scratch_shapes=[
            pltpu.VMEM((8, units), f32),
            pltpu.VMEM((4 * lines + 1, rows, dim), bf16),
            pltpu.VMEM((dim, width), bf16),
            pltpu.VMEM((dim, width), bf16),
            pltpu.VMEM((2, lines * 2 * rows, dim), bf16),
            pltpu.VMEM((2, lines * 2 * rows, width), bf16),
            pltpu.VMEM((2, lines, 2 * rows, columns), bf16),
            pltpu.VMEM((2, lines, 2 * rows, columns), f32),
            pltpu.VMEM((2, lines, 2 * rows, columns), bf16),
            pltpu.VMEM((2, lines, 2 * rows, columns), bf16),
            pltpu.VMEM((2, lines, 2 * rows, columns), bf16),
            pltpu.VMEM((3, rows, columns), bf16),
            pltpu.VMEM((2, rows, columns), f32),
            pltpu.VMEM((3, rows, columns), bf16),
            dma((2, lines, 2)),
            dma((4,)),
            dma((4,)),
            dma((2, lines)),
            dma((2, lines)),
            dma((2,)),
            dma((3,)),
            dma((n_sends,)),
        ],
        compiler_params=pltpu.CompilerParams(
            collective_id=0, has_side_effects=True, vmem_limit_bytes=VMEM_GRANT
        ),
    )(tokens, gain[None], bias[None], w_in, b_in[None], w_out.T, b_out[None]).astype(bf16)


def gathered(tokens, norm_gain, norm_bias, w_in, b_in, w_out, b_out):
    values = tokens.astype(jnp.float32)
    center = jnp.mean(values, axis=1, keepdims=True)
    spread = jnp.mean((values - center) ** 2, axis=1, keepdims=True)
    normed = ((values - center) / jnp.sqrt(spread + 1e-06) * norm_gain + norm_bias).astype(
        jnp.bfloat16
    )
    w_in_full = lax.all_gather(w_in, "dp", axis=0, tiled=True)
    everyone = lax.all_gather(normed, "mp", axis=0, tiled=True)
    pre = jnp.dot(everyone, w_in_full, preferred_element_type=jnp.float32) + b_in
    hidden = jax.nn.gelu(pre, approximate=False).astype(jnp.bfloat16)
    w_out_full = lax.all_gather(w_out, "dp", axis=1, tiled=True)
    summed = lax.psum_scatter(
        jnp.dot(hidden, w_out_full, preferred_element_type=jnp.float32),
        "mp",
        scatter_dimension=0,
        tiled=True,
    )
    return (values + summed + b_out).astype(jnp.bfloat16)


def on_device(dp, mp, tokens, norm_gain, norm_bias, w_in, b_in, w_out, b_out):
    rows, (depth, units) = tokens.shape[0], w_in.shape
    fits = (
        dp == 4
        and mp % 2 == 0
        and mp & (mp - 1) == 0
        and units % LANES == 0
        and depth % 16 == 0
        and 2 * depth % LANES == 0
        and rows % 8 == 0
        and mp * 2 * rows * (2 * depth) * 2 * 24 < VMEM_GRANT
    )
    if fits:
        return fused(mp, tokens, norm_gain, norm_bias, w_in, b_in, w_out, b_out)
    return gathered(tokens, norm_gain, norm_bias, w_in, b_in, w_out, b_out)


def solution(mesh):
    placed = (P(("dp", "mp"), None), P(), P(), P("dp", "mp"), P("mp"), P("mp", "dp"), P())
    return jax.shard_map(
        functools.partial(on_device, mesh.shape["dp"], mesh.shape["mp"]),
        mesh=mesh,
        in_specs=placed,
        out_specs=P(("dp", "mp"), None),
        check_vma=False,
    )
```

time: 249 us -> 91.4 us (0.37)
  waiting for transfers between devices: 215 us -> 0 us
  Pallas kernels: 0 us -> 84.1 us
  matrix products: 15.7 us -> 0 us
  between operations: 13.2 us -> 0.01 us
  local copies, waits for them, and re-layouts: 0.02 us -> 5.18 us
  other arithmetic: 5.56 us -> 1.63 us
    all_gather x3 -> x0, waiting for transfers between devices: 144 us -> none  [the longest x1 51.3 us: on_device(): w_out_full = lax.all_gather(w_out, 'dp', axis=1, tiled=True)]
    pallas_call x0 -> x1, Pallas kernels: none -> 84.1 us  [fused(): pl.pallas_call(functools.partial(kernel, lines), out_shape=jax.ShapeDtype...]
    reduce_scatter x1 -> x0, waiting for transfers between devices: 69.7 us -> none  [on_device(): lax.psum_scatter(jnp.dot(hidden, w_out_full, preferred_element_type=jnp.f...]
    dot_general x1 -> x0, matrix products: 15.7 us -> none  [on_device(): jnp.dot(hidden, w_out_full, preferred_element_type=jnp.float32)]
    broadcast_in_dim x0 -> x4, local copies, waits for them, and re-layouts: none -> 5.18 us  [the longest x1 1.3 us: fused(): gain[None]]
  transfers between devices with their start and end apart: 4 -> 0, of which waited for: 4 -> 0; matrix products, arithmetic and copies ran while one was open for 0% -> 0% of each run, Pallas kernels for 0% -> 0%
where the time goes in v1:
time: 91.4 us; the launch traced here: 90.9 us
  Pallas kernels  84.1 us (92%)
  local copies, waits for them, and re-layouts  5.18 us (6%)
  other arithmetic  1.63 us (2%)
    pallas_call x1, Pallas kernels, fused(): pl.pallas_call(functools.partial(kernel, lines), out_shape=jax.ShapeDtype...  84.1 us

profile of v1, /device:TPU:0, one launch (start us, length us, event | category | flops | bytes accessed | tf_op | source)
XLA Modules:
  0.0 90.9 jit_solution(13100046481779803007)
XLA Ops:
  0.0 1.3 %broadcast_in_dim.12.gain = f32[1,1792]{1,0:T(1,128)} reshape(f32[1792]{0:T(1024)} %param.8) | data formatting | bytes 14336 | tf_op jit(solution)/shard_map/broadcast_in_dim | solution.py:260
  1.3 1.3 %broadcast_in_dim.13.bias = f32[1,1792]{1,0:T(1,128)} reshape(f32[1792]{0:T(1024)} %param.9) | data formatting | bytes 14336 | tf_op jit(solution)/shard_map/broadcast_in_dim | solution.py:260
  2.6 1.3 %broadcast_in_dim.15.b_out = f32[1,1792]{1,0:T(1,128)} reshape(f32[1792]{0:T(1024)} %param.13) | data formatting | bytes 14336 | tf_op jit(solution)/shard_map/broadcast_in_dim | solution.py:260
  3.9 1.3 %broadcast_in_dim.14.b_in = f32[1,1920]{1,0:T(1,128)} reshape(f32[1920]{0:T(1024)} %param.11) | data formatting | bytes 15360 | tf_op jit(solution)/shard_map/broadcast_in_dim | solution.py:260
  5.2 84.1 %shard_map.73 = f32[40,1792]{1,0:T(8,128)} custom-call(bf16[40,1792]{1,0:T(8,128)(2,1)} %tokens.1, f32[1,1792]{1,0:T(1,128)} %broadcast_in_dim.12.gain, f32[1,1792]{1,0:T(1,128)} %broadcast_in_dim.13.bias, bf16[448,1920]{1,0:T(8,128)(2,1)} %w_in.1, f32[1,1920]{1,0:T(1,128)} %broadcast_in_dim.14.b_in, bf16[448,1920]{1,0:T(8,128)(2,1)} %bitcast.1, ...), custom_call_target="tpu_custom_call" | custom-call | tf_op jit(solution)/shard_map/pallas_call | solution.py:228
  89.3 1.6 %convert_element_type.3 = bf16[40,1792]{1,0:T(8,128)(2,1)} convert(f32[40,1792]{1,0:T(8,128)} %shard_map.73) | non-fusion elementwise | flops 71680 | bytes 430080 | tf_op jit(solution)/shard_map/convert_element_type | solution.py:260

commit v2 on v1

--- a/solution.py
+++ b/solution.py
@@ -132,27 +132,6 @@
 
         lax.fori_loop(0, width // tile, step, 0)
 
-    locals_[0].wait()
-
-    def norm_own(zz, carry):
-        normalise(y, zz)
-        return carry
-
-    lax.fori_loop(0, lines, norm_own, 0)
-
-    arrive(rows_of(win, far), win_sem.at[far])
-    send(rows_of(win, far), rows_of(win, far), win_sem.at[far], core_dev)
-    locals_[1].wait()
-    arrive(rows_of(win, near), win_sem.at[near])
-    arrive(rows_of(win, across), win_sem.at[across])
-    first(y)
-
-    for k in range(lines):
-        for side in (x, ox):
-            arrive(tok.at[slot(oy, z_at[k], side)], tok_sem.at[oy, z_at[k], side])
-        normalise(oy, z_at[k])
-    first(oy)
-
     def second(q, yy, zz):
         side = x if q == 0 else ox
         act = hidden[yy, pl.ds(pl.multiple_of(zz * 2 * rows, 16), 2 * rows), :]
@@ -166,11 +145,36 @@
             part[q, z_at[k]] = second(q, oy, z_at[k]).astype(part.dtype)
             send(part.at[q, z_at[k]], from_y.at[q, z_at[k]], y_sem.at[q, z_at[k]], y_dev)
 
+    def product_own(q):
         def step(zz, carry):
             own[q, zz] = second(q, y, zz)
             return carry
 
         lax.fori_loop(0, lines, step, 0)
+
+    locals_[0].wait()
+
+    def norm_own(zz, carry):
+        normalise(y, zz)
+        return carry
+
+    lax.fori_loop(0, lines, norm_own, 0)
+
+    arrive(rows_of(win, far), win_sem.at[far])
+    send(rows_of(win, far), rows_of(win, far), win_sem.at[far], core_dev)
+    locals_[1].wait()
+    arrive(rows_of(win, near), win_sem.at[near])
+    arrive(rows_of(win, across), win_sem.at[across])
+    first(y)
+    locals_[2].wait()
+    arrive(rows_of(wout, near), wout_sem.at[near])
+    product_own(0)
+
+    for k in range(lines):
+        for side in (x, ox):
+            arrive(tok.at[slot(oy, z_at[k], side)], tok_sem.at[oy, z_at[k], side])
+        normalise(oy, z_at[k])
+    first(oy)
 
     def along_z(q):
         for k in list(range(1, lines)) + [0]:
@@ -194,14 +198,13 @@
         send(to_x.at[q], from_x.at[side], x_sem.at[side], x_dev)
         kept[side] = own[q, z, pl.ds(pl.multiple_of(x * rows, 8), rows), :]
 
-    locals_[2].wait()
-    arrive(rows_of(wout, near), wout_sem.at[near])
     product(0)
     arrive(rows_of(wout, far), wout_sem.at[far])
     send(rows_of(wout, far), rows_of(wout, far), wout_sem.at[far], core_dev)
     along_z(0)
     arrive(rows_of(wout, across), wout_sem.at[across])
     product(1)
+    product_own(1)
     along_x(0)
     along_z(1)
     along_x(1)

time: 91.4 us -> 93.8 us (1.026)
  Pallas kernels: 84.1 us -> 86 us
    pallas_call x1, Pallas kernels: 84.1 us -> 86 us  [fused(): pl.pallas_call(functools.partial(kernel, lines), out_shape=jax.ShapeDtype...]
where the time goes in v2:
time: 93.8 us; the launch traced here: 92.8 us
  Pallas kernels  86 us (92%)
  local copies, waits for them, and re-layouts  5.18 us (6%)
  other arithmetic  1.63 us (2%)
    pallas_call x1, Pallas kernels, fused(): pl.pallas_call(functools.partial(kernel, lines), out_shape=jax.ShapeDtype...  86 us

profile of v2, /device:TPU:0, one launch (start us, length us, event | category | flops | bytes accessed | tf_op | source)
XLA Modules:
  0.0 92.8 jit_solution(9732934469296901805)
XLA Ops:
  0.0 1.3 %broadcast_in_dim.12.gain = f32[1,1792]{1,0:T(1,128)} reshape(f32[1792]{0:T(1024)} %param.8) | data formatting | bytes 14336 | tf_op jit(solution)/shard_map/broadcast_in_dim | solution.py:263
  1.3 1.3 %broadcast_in_dim.13.bias = f32[1,1792]{1,0:T(1,128)} reshape(f32[1792]{0:T(1024)} %param.9) | data formatting | bytes 14336 | tf_op jit(solution)/shard_map/broadcast_in_dim | solution.py:263
  2.6 1.3 %broadcast_in_dim.15.b_out = f32[1,1792]{1,0:T(1,128)} reshape(f32[1792]{0:T(1024)} %param.13) | data formatting | bytes 14336 | tf_op jit(solution)/shard_map/broadcast_in_dim | solution.py:263
  3.9 1.3 %broadcast_in_dim.14.b_in = f32[1,1920]{1,0:T(1,128)} reshape(f32[1920]{0:T(1024)} %param.11) | data formatting | bytes 15360 | tf_op jit(solution)/shard_map/broadcast_in_dim | solution.py:263
  5.2 86.0 %shard_map.73 = f32[40,1792]{1,0:T(8,128)} custom-call(bf16[40,1792]{1,0:T(8,128)(2,1)} %tokens.1, f32[1,1792]{1,0:T(1,128)} %broadcast_in_dim.12.gain, f32[1,1792]{1,0:T(1,128)} %broadcast_in_dim.13.bias, bf16[448,1920]{1,0:T(8,128)(2,1)} %w_in.1, f32[1,1920]{1,0:T(1,128)} %broadcast_in_dim.14.b_in, bf16[448,1920]{1,0:T(8,128)(2,1)} %bitcast.1, ...), custom_call_target="tpu_custom_call" | custom-call | tf_op jit(solution)/shard_map/pallas_call | solution.py:231
  91.1 1.6 %convert_element_type.3 = bf16[40,1792]{1,0:T(8,128)(2,1)} convert(f32[40,1792]{1,0:T(8,128)} %shard_map.73) | non-fusion elementwise | flops 71680 | bytes 430080 | tf_op jit(solution)/shard_map/convert_element_type | solution.py:263
